TPU v7x, 32 devices: a whole 2x2x4 slice. The times are simulated.
32 devices in a mesh: dp: 8 (over z, y), tensor: 4 (over x, core).
Axes of the slice: x: 2, y: 2, z: 4, core: 2. Of those that a mesh axis runs over, the one named last changes fastest.
Arguments:
- tokens: bfloat16 [16384, 768], P(('dp', 'tensor')), may hold values from -6 to 6
- seq_lengths: int32 [16], P('dp'), may hold values from 100 to 1024, as said below
- cotangent: bfloat16 [16384, 768], P(('dp', 'tensor')), may hold values from -6 to 6
- ln1_gain: bfloat16 [768], replicated, may hold values from 0.5 to 1.5
- ln1_shift: bfloat16 [768], replicated, may hold values from -2 to 2
- w_qkv: bfloat16 [768, 3, 768], P(None, None, 'tensor'), may hold values from -0.21875 to 0.21875
- b_qkv: bfloat16 [3, 768], P(None, 'tensor'), may hold values from -2 to 2
- w_out: bfloat16 [768, 768], P('tensor'), may hold values from -1.25 to 1.25
- b_out: bfloat16 [768], replicated, may hold values from -2 to 2
- ln2_gain: bfloat16 [768], replicated, may hold values from 0.5 to 1.5
- ln2_shift: bfloat16 [768], replicated, may hold values from -2 to 2
- w_up: bfloat16 [768, 3072], P(None, 'tensor'), may hold values from -0.21875 to 0.21875
- b_up: bfloat16 [3072], P('tensor'), may hold values from -2 to 2
- w_down: bfloat16 [3072, 768], P('tensor'), may hold values from -0.109375 to 0.109375
- b_down: bfloat16 [768], replicated, may hold values from -2 to 2
Outputs:
- output: bfloat16 [16384, 768], P(('dp', 'tensor'))
- grad_tokens: bfloat16 [16384, 768], P(('dp', 'tensor'))
- grad_ln1_gain: float32 [768], replicated
- grad_ln1_shift: float32 [768], replicated
- grad_w_qkv: float32 [768, 3, 768], P(None, None, 'tensor')
- grad_b_qkv: float32 [3, 768], P(None, 'tensor')
- grad_w_out: float32 [768, 768], P('tensor')
- grad_b_out: float32 [768], replicated
- grad_ln2_gain: float32 [768], replicated
- grad_ln2_shift: float32 [768], replicated
- grad_w_up: float32 [768, 3072], P(None, 'tensor')
- grad_b_up: float32 [3072], P('tensor')
- grad_w_down: float32 [3072, 768], P('tensor')
- grad_b_down: float32 [768], replicated
Inputs may be any that keep to these rules, and one draw needn't show every extreme that they name: `seq_lengths`: number of codons of each sequence; one sequence has exactly 1024 and one exactly 100; short sequences are more common than long ones.
All inputs are finite; a program needn't handle non-finite values.
Results may differ from a plain program's by a relative error of at most 0.013.
Values may be sent and summed in bfloat16 or wider, within the bound.
A program may use at most 128 MiB of HBM per device.

v0:
```python
import math
import jax
import jax.numpy as jnp
from jax import lax
from jax.sharding import PartitionSpec as P

HEAD_DIM = 64
SEQ = 1024
norm_eps = 1e-05
mask_fill = -1e30


def layer_norm(values, ln_gain, ln_shift):
    row_mean = jnp.mean(values, axis=-1, keepdims=True)
    centred = values - row_mean
    row_var = jnp.mean(centred * centred, axis=-1, keepdims=True)
    return centred * lax.rsqrt(row_var + norm_eps) * ln_gain + ln_shift


def rotary_tables():
    half_dim = HEAD_DIM // 2
    inverse_freq = jnp.exp(
        jnp.arange(half_dim, dtype=jnp.float32) * (-2.0 * math.log(10000.0) / HEAD_DIM)
    )
    angles = jnp.arange(SEQ, dtype=jnp.float32)[:, None] * inverse_freq[None, :]
    return (jnp.cos(angles), jnp.sin(angles))


def rotate(head_vals, cosine, sine_table):
    half_dim = head_vals.shape[-1] // 2
    lower_half = head_vals[..., :half_dim]
    upper_half = head_vals[..., half_dim:]
    cos_part = cosine[:, None, :]
    sin_part = sine_table[:, None, :]
    return jnp.concatenate(
        [
            lower_half * cos_part - upper_half * sin_part,
            upper_half * cos_part + lower_half * sin_part,
        ],
        axis=-1,
    )


def contract_last(left_mat, right_mat):
    return lax.dot_general(
        left_mat, right_mat, (((1,), (1,)), ((), ())), preferred_element_type=jnp.float32
    )


def contract_first(left_mat, right_mat):
    return lax.dot_general(
        left_mat, right_mat, (((0,), (0,)), ((), ())), preferred_element_type=jnp.float32
    )


def local(
    tokens,
    seq_lengths,
    cotangent,
    ln1_gain,
    ln1_shift,
    w_qkv,
    b_qkv,
    w_out,
    b_out,
    ln2_gain,
    ln2_shift,
    w_up,
    b_up,
    w_down,
    b_down,
):
    local_rows = tokens.shape[0]
    group_rows = local_rows * lax.axis_size("tensor")
    seq_count = seq_lengths.shape[0]
    qkv_width = w_qkv.shape[2]
    local_heads = qkv_width // HEAD_DIM
    head_scale = HEAD_DIM ** (-0.5)
    block_rows = min(512, SEQ)
    cosine, sine_table = rotary_tables()
    resid = tokens.astype(jnp.float32)
    normed_one, norm_one_back = jax.vjp(
        layer_norm, resid, ln1_gain.astype(jnp.float32), ln1_shift.astype(jnp.float32)
    )
    normed_one_low = normed_one.astype(jnp.bfloat16)
    normed_all = lax.all_gather(normed_one_low, "tensor", axis=0, tiled=True)
    qkv_pre = jnp.einsum(
        "td,dcf->tcf", normed_all, w_qkv, preferred_element_type=jnp.float32
    ) + b_qkv.astype(jnp.float32)

    def split_heads(matrix):
        return matrix.reshape(seq_count, SEQ, local_heads, HEAD_DIM)

    def rotate_pair(query_raw, key_raw):
        return (rotate(query_raw, cosine, sine_table), rotate(key_raw, cosine, sine_table))

    (query_rot, key_rot), rotate_back = jax.vjp(
        rotate_pair, split_heads(qkv_pre[:, 0]), split_heads(qkv_pre[:, 1])
    )
    query_low = query_rot.astype(jnp.bfloat16)
    key_low = key_rot.astype(jnp.bfloat16)
    value_low = split_heads(qkv_pre[:, 2]).astype(jnp.bfloat16)

    def attend_fwd(inputs):
        query_seq, key_seq, value_seq, seq_len = inputs
        key_valid = jnp.arange(SEQ) < seq_len
        out_parts = []
        lse_parts = []
        for offset in range(0, SEQ, block_rows):
            query_blk = query_seq[offset : offset + block_rows]
            scores = (
                jnp.einsum("qhe,khe->hqk", query_blk, key_seq, preferred_element_type=jnp.float32)
                * head_scale
            )
            scores = jnp.where(key_valid[None, None, :], scores, mask_fill)
            row_max = jnp.max(scores, axis=-1, keepdims=True)
            shifted = jnp.exp(scores - row_max)
            row_total = jnp.sum(shifted, axis=-1, keepdims=True)
            weights = (shifted / row_total).astype(jnp.bfloat16)
            out_parts.append(
                jnp.einsum("hqk,khe->qhe", weights, value_seq, preferred_element_type=jnp.float32)
            )
            lse_parts.append((row_max + jnp.log(row_total))[..., 0])
        return (jnp.concatenate(out_parts, axis=0), jnp.concatenate(lse_parts, axis=1))

    attended, log_sums = lax.map(attend_fwd, (query_low, key_low, value_low, seq_lengths))
    attn_vals = attended.reshape(group_rows, qkv_width).astype(jnp.bfloat16)
    mixed = (
        resid
        + lax.psum_scatter(
            jnp.dot(
                lax.slice_in_dim(attn_vals, 0, local_rows * lax.axis_size("tensor"), axis=0),
                w_out,
                preferred_element_type=jnp.float32,
            ),
            "tensor",
            scatter_dimension=0,
            tiled=True,
        )
        + b_out.astype(jnp.float32)
    )
    normed_two, norm_two_back = jax.vjp(
        layer_norm, mixed, ln2_gain.astype(jnp.float32), ln2_shift.astype(jnp.float32)
    )
    normed_two_low = normed_two.astype(jnp.bfloat16)
    grad_out = cotangent.astype(jnp.float32)
    normed_two_all = lax.all_gather(normed_two_low, "tensor", axis=0, tiled=True)
    pre_act = jnp.dot(normed_two_all, w_up, preferred_element_type=jnp.float32) + b_up.astype(
        jnp.float32
    )
    act_vals, gelu_back = jax.vjp(jax.nn.gelu, pre_act)
    act_low = act_vals.astype(jnp.bfloat16)
    ffn_vals = lax.psum_scatter(
        jnp.dot(
            lax.slice_in_dim(act_low, 0, local_rows * lax.axis_size("tensor"), axis=0),
            w_down,
            preferred_element_type=jnp.float32,
        ).astype(jnp.bfloat16),
        "tensor",
        scatter_dimension=0,
        tiled=True,
    ).astype(jnp.float32)
    output = (mixed + ffn_vals + b_down.astype(jnp.float32)).astype(jnp.bfloat16)
    cot_all = lax.all_gather(cotangent, "tensor", axis=0, tiled=True)
    d_act = contract_last(cot_all, w_down)
    grad_w_down = contract_first(act_low, cot_all)
    d_pre = gelu_back(d_act)[0].astype(jnp.bfloat16)
    grad_w_up = contract_first(normed_two_all, d_pre)
    grad_b_up = jnp.sum(d_pre.astype(jnp.float32), axis=0)
    d_normed_two = lax.psum_scatter(
        contract_last(
            lax.slice_in_dim(d_pre, 0, local_rows * lax.axis_size("tensor"), axis=0), w_up
        ),
        "tensor",
        scatter_dimension=0,
        tiled=True,
    )
    d_mixed_norm, grad_gain_two, grad_shift_two = norm_two_back(d_normed_two)
    d_mixed = grad_out + d_mixed_norm
    d_branch = d_mixed.astype(jnp.bfloat16)
    branch_all = lax.all_gather(d_branch, "tensor", axis=0, tiled=True)
    grad_w_out = contract_first(attn_vals, branch_all)
    d_vals = contract_last(branch_all, w_out).astype(jnp.bfloat16)

    def attend_back(inputs):
        query_seq, key_seq, value_seq, dout_seq, lse_seq, seq_len = inputs
        key_valid = jnp.arange(SEQ) < seq_len
        dquery_parts = []
        dkey_sum = jnp.zeros(key_seq.shape, jnp.float32)
        dvalue_sum = jnp.zeros(value_seq.shape, jnp.float32)
        for offset in range(0, SEQ, block_rows):
            query_blk = query_seq[offset : offset + block_rows]
            dout_blk = dout_seq[offset : offset + block_rows]
            lse_blk = lse_seq[:, offset : offset + block_rows]
            scores = (
                jnp.einsum("qhe,khe->hqk", query_blk, key_seq, preferred_element_type=jnp.float32)
                * head_scale
            )
            scores = jnp.where(key_valid[None, None, :], scores, mask_fill)
            probs = jnp.exp(scores - lse_blk[:, :, None])
            weights = probs.astype(jnp.bfloat16)
            dvalue_sum = dvalue_sum + jnp.einsum(
                "hqk,qhe->khe", weights, dout_blk, preferred_element_type=jnp.float32
            )
            d_probs = jnp.einsum(
                "qhe,khe->hqk", dout_blk, value_seq, preferred_element_type=jnp.float32
            )
            inner_sum = jnp.sum(probs * d_probs, axis=-1, keepdims=True)
            d_scores = (probs * (d_probs - inner_sum)).astype(jnp.bfloat16)
            dquery_parts.append(
                jnp.einsum("hqk,khe->qhe", d_scores, key_seq, preferred_element_type=jnp.float32)
                * head_scale
            )
            dkey_sum = (
                dkey_sum
                + jnp.einsum(
                    "hqk,qhe->khe", d_scores, query_blk, preferred_element_type=jnp.float32
                )
                * head_scale
            )
        return (jnp.concatenate(dquery_parts, axis=0), dkey_sum, dvalue_sum)

    d_query, d_key, d_values = lax.map(
        attend_back, (query_low, key_low, value_low, split_heads(d_vals), log_sums, seq_lengths)
    )
    d_query_raw, d_key_raw = rotate_back((d_query, d_key))
    d_qkv = jnp.stack(
        [
            d_query_raw.reshape(group_rows, qkv_width),
            d_key_raw.reshape(group_rows, qkv_width),
            d_values.reshape(group_rows, qkv_width),
        ],
        axis=1,
    ).astype(jnp.bfloat16)
    grad_w_qkv = jnp.einsum("td,tcf->dcf", normed_all, d_qkv, preferred_element_type=jnp.float32)
    grad_b_qkv = jnp.sum(d_qkv.astype(jnp.float32), axis=0)
    d_normed_one = lax.psum_scatter(
        jnp.einsum(
            "tcf,dcf->td",
            lax.slice_in_dim(d_qkv, 0, local_rows * lax.axis_size("tensor"), axis=0),
            w_qkv,
            preferred_element_type=jnp.float32,
        ),
        "tensor",
        scatter_dimension=0,
        tiled=True,
    )
    d_resid_norm, grad_gain_one, grad_shift_one = norm_one_back(d_normed_one)
    grad_tokens = (d_mixed + d_resid_norm).astype(jnp.bfloat16)
    grad_w_qkv, grad_b_qkv, grad_w_out, grad_w_up, grad_b_up, grad_w_down = lax.psum(
        (grad_w_qkv, grad_b_qkv, grad_w_out, grad_w_up, grad_b_up, grad_w_down), "dp"
    )
    shared_local = jnp.stack(
        [
            grad_gain_one,
            grad_shift_one,
            jnp.sum(d_mixed, axis=0),
            grad_gain_two,
            grad_shift_two,
            jnp.sum(grad_out, axis=0),
        ]
    )
    shared_sum = lax.psum(shared_local, ("dp", "tensor"))
    return (
        output,
        grad_tokens,
        shared_sum[0],
        shared_sum[1],
        grad_w_qkv,
        grad_b_qkv,
        grad_w_out,
        shared_sum[2],
        shared_sum[3],
        shared_sum[4],
        grad_w_up,
        grad_b_up,
        grad_w_down,
        shared_sum[5],
    )


def solution(mesh):
    placed = (
        P(("dp", "tensor"), None),
        P("dp"),
        P(("dp", "tensor"), None),
        P(),
        P(),
        P(None, None, "tensor"),
        P(None, "tensor"),
        P("tensor", None),
        P(),
        P(),
        P(),
        P(None, "tensor"),
        P("tensor"),
        P("tensor", None),
        P(),
    )
    return jax.shard_map(
        local,
        mesh=mesh,
        in_specs=placed,
        out_specs=(
            P(("dp", "tensor"), None),
            P(("dp", "tensor"), None),
            P(),
            P(),
            P(None, None, "tensor"),
            P(None, "tensor"),
            P("tensor", None),
            P(),
            P(),
            P(),
            P(None, "tensor"),
            P("tensor"),
            P("tensor", None),
            P(),
        ),
        check_vma=False,
    )
```

profile of v0, /device:TPU:0, one launch (start us, length us, event | category | flops | bytes accessed | tf_op | source)
XLA Modules:
  0.0 759.7 jit_solution(15909219942713301804)
XLA Ops:
  17.8 28.2 %all-gather.5.cloned.1.call-done = bf16[2048,768]{1,0:T(8,128)(2,1)} async-done(((bf16[512,768]{1,0:T(8,128)(2,1)}), bf16[2048,768]{1,0:T(8,128)(2,1)}) %all-gather.5.cloned.1.call-update) | async-done | bytes 3145744 | tf_op jit(solution)/shard_map/all_gather | solution.py:86
  46.0 3.9 fusion.118
  52.2 2.8 reshape_squeeze.8
  64.9 24.7 %while.28 = (s32[]{:T(128)}, bf16[2,1024,3,64]{1,3,2,0:T(8,128)(2,1)}, f32[2,3,1024]{2,1,0:T(4,128)}, bf16[2,1024,3,64]{1,3,2,0:T(8,128)(2,1)S(1)}, s32[2]{0:T(1...) while((s32[]{:T(128)}, ...), condition=%wide.region_7.8_spmd.clone, body=%wide.region_2.7_spmd.sunk.clone | while | flops 843842560 | bytes 47532784 | solution.py:126
  92.9 3.7 fusion.119
  98.0 57.6 %reduce-scatter.5.cloned.1.call-done = f32[512,768]{1,0:T(8,128)} async-done(((f32[2048,768]{1,0:T(8,128)}), f32[512,768]{1,0:T(8,128)}) %reduce-scatter.5.cloned.1.call-update) | async-done | bytes 1572880 | tf_op jit(solution)/shard_map/reduce_scatter | solution.py:130
  160.4 28.0 %all-gather.7.cloned.1.call-done = bf16[2048,768]{1,0:T(8,128)(2,1)} async-done(((bf16[512,768]{1,0:T(8,128)(2,1)}), bf16[2048,768]{1,0:T(8,128)(2,1)}) %all-gather.7.cloned.1.call-update) | async-done | bytes 3145744 | tf_op jit(solution)/shard_map/all_gather | solution.py:147
  188.4 7.5 fusion.120
  195.9 22.5 %all-gather.9.cloned.1.call-done = bf16[2048,768]{1,0:T(8,128)(2,1)} async-done(((bf16[512,768]{1,0:T(8,128)(2,1)}), bf16[2048,768]{1,0:T(8,128)(2,1)}) %all-gather.9.cloned.1.call-update) | async-done | bytes 3145744 | tf_op jit(solution)/shard_map/all_gather | solution.py:164
  218.3 12.4 %convert_reduce_fusion = (f32[768]{0:T(1024)}, bf16[2048,768]{1,0:T(8,128)(2,1)S(1)}, bf16[2048,768]{1,0:T(8,128)(2,1)}) fusion(f32[2048,768]{1,0:T(8,128)} %fusion.120, f32[768]{0:T(1024)S(1)} %convert_element_type.109, bf16[2048,768]{1,0:T(8,128)(2,1)} %all-gather.9.cloned.1.call-done, bf16[768,768]{1,0:T(8,128)(2,1)S(1)} %copy-done), kind=kOutput, calls=%fused_computation.112 | convolution fusion | flops 2455239936 | bytes 16914432 | tf_op jit(solution)/shard_map/dot_general | solution.py:45
  232.5 4.5 fusion.121
  237.1 6.5 convolution_convert_fusion
  244.3 51.7 %reduce-scatter.9.cloned.1.call-done = f32[512,768]{1,0:T(8,128)} async-done(((f32[2048,768]{1,0:T(8,128)}), f32[512,768]{1,0:T(8,128)}) %reduce-scatter.9.cloned.1.call-update) | async-done | bytes 1572880 | tf_op jit(solution)/shard_map/reduce_scatter | solution.py:170
  296.1 3.1 multiply_reduce_fusion.2
  299.2 37.2 %reduce-scatter.7.cloned.1.call-done = bf16[512,768]{1,0:T(8,128)(2,1)} async-done(((bf16[2048,768]{1,0:T(8,128)(2,1)}), bf16[512,768]{1,0:T(8,128)(2,1)}) %reduce-scatter.7.cloned.1.call-update) | async-done | bytes 786448 | tf_op jit(solution)/shard_map/reduce_scatter | solution.py:153
  336.4 3.7 fusion.110
  342.6 28.4 %all-gather.11.cloned.1.call-done = bf16[2048,768]{1,0:T(8,128)(2,1)} async-done(((bf16[512,768]{1,0:T(8,128)(2,1)}), bf16[2048,768]{1,0:T(8,128)(2,1)}) %all-gather.11.cloned.1.call-update) | async-done | bytes 3145744 | tf_op jit(solution)/shard_map/all_gather | solution.py:181
  371.0 3.1 convolution_convert_fusion.1
  376.9 56.3 %while.29 = (s32[]{:T(128)}, f32[2,1024,3,64]{1,3,2,0:T(8,128)}, f32[2,1024,3,64]{1,3,2,0:T(8,128)}, bf16[2,1024,3,64]{1,3,2,0:T(8,128)(2,1)S(1)}, bf16[2,1024,3...) while((s32[]{:T(128)}, f32[2,1024,3,64]{1,3,2,0:T(8,128)}, ...), condition=%wide.region_18.19_spmd.clone, body=%wide.region_15.18_spmd.sunk.clone | while | flops 2061432832 | bytes 165286976 | solution.py:223
  387.6 4.8 multiply_reduce_fusion.7
  392.5 4.0 multiply_convert_fusion.5
  415.7 4.8 multiply_reduce_fusion.7
  420.5 4.0 multiply_convert_fusion.5
  444.3 4.6 convolution_bitcast_fusion
  449.3 7.1 fusion.124
  456.3 4.2 fusion.123
  462.8 3.2 fusion.125
  469.0 22.1 %all-reduce.4 = (f32[3,192]{1,0:T(4,128)}, f32[768]{0:T(1024)}) all-reduce(f32[3,192]{1,0:T(4,128)S(1)} %convert_reduce_fusion.1, f32[768]{0:T(1024)S(1)} %copy-done.56), channel_id=1, replica_groups=mesh['dp'=8,'tensor'=4] {'dp'}, use_global_device_ids=true, to_apply=%region_31.32 | all-reduce | flops 1344 | bytes 10752 | tf_op jit(solution)/shard_map/psum | solution.py:250
  491.2 16.8 %reduce-scatter.11.cloned.1.call-done = f32[512,768]{1,0:T(8,128)} async-done(((f32[2048,768]{1,0:T(8,128)}), f32[512,768]{1,0:T(8,128)}) %reduce-scatter.11.cloned.1.call-update) | async-done | bytes 1572880 | tf_op jit(solution)/shard_map/reduce_scatter | solution.py:237
  512.6 43.9 %psum.49 = f32[6,768]{1,0:T(8,128)S(1)} all-reduce(f32[6,768]{1,0:T(8,128)S(1)} %stack.20), channel_id=1, replica_groups=mesh['dp'=8,'tensor'=4] {'dp','tensor'}, use_global_device_ids=true, to_apply=%region_28.29 | all-reduce | flops 4608 | bytes 36864 | tf_op jit(solution)/shard_map/psum | solution.py:263
  557.1 189.1 %all-reduce.8.cloned.1.call-done = (f32[768,3,192]{0,2,1:T(8,128)}, f32[192,768]{1,0:T(8,128)}, f32[768,768]{1,0:T(8,128)}, f32[768,768]{1,0:T(8,128)}) async-done(((f32[768,3,192]{0,2,1:T(8,128)}, f32[192,768]{1,0:T(8,128)}, f32[768,768]{1,0:T(8,128)}, f32[768,768]{1,0:T(8,128)}), (f32[768,3,192]{0,2,1:T(8,128)}, f32[192,768]{1,0:T(8,128)}, f32[768,768]{1,0:T(8,128)}, ...) | async-done | bytes 7077904 | tf_op jit(solution)/shard_map/psum | solution.py:250
  746.3 2.9 copy.97
  (314 shorter events, 127.2 us)
Async XLA Ops:
  7.2 211.2 %copy-start = (bf16[768,768]{1,0:T(8,128)(2,1)S(1)}, bf16[768,768]{1,0:T(8,128)(2,1)}, u32[]{:S(2)}) copy-start(bf16[768,768]{1,0:T(8,128)(2,1)} %param.32) | copy-start | bytes 3538948
  7.2 7.5 copy-start.57
  7.2 38.8 %copy-start.65 = (bf16[768,3,192]{0,2,1:T(8,128)(2,1)S(1)}, bf16[768,3,192]{0,2,1:T(8,128)(2,1)}, u32[]{:S(2)}) copy-start(bf16[768,3,192]{0,2,1:T(8,128)(2,1)} %param.24) | copy-start | bytes 2654212
  7.2 38.8 %all-gather.5.cloned.1.call-start = ((), (), s32[]{:S(2)}) async-start(), calls=%async_computation.4 | async-start | bytes 3932160 | tf_op jit(solution)/shard_map/all_gather | solution.py:86
  14.6 141.1 %reduce-scatter.5.cloned.1.call-start = ((), (), s32[]{:S(2)}) async-start(), calls=%async_computation.5 | async-start | bytes 7864320 | tf_op jit(solution)/shard_map/reduce_scatter | solution.py:130
  96.6 59.0 %copy-start.7 = (bf16[512,768]{1,0:T(8,128)(2,1)S(1)}, bf16[512,768]{1,0:T(8,128)(2,1)}, u32[]{:S(2)}) copy-start(bf16[512,768]{1,0:T(8,128)(2,1)} %param.19) | copy-start | bytes 2359300
  96.7 91.7 %all-gather.7.cloned.1.call-start = ((), (), s32[]{:S(2)}) async-start(), calls=%async_computation.6 | async-start | bytes 3932160 | tf_op jit(solution)/shard_map/all_gather | solution.py:147
  159.7 58.6 %all-gather.9.cloned.1.call-start = ((), (), s32[]{:S(2)}) async-start(), calls=%async_computation.8 | async-start | bytes 3932160 | tf_op jit(solution)/shard_map/all_gather | solution.py:164
  160.3 135.8 %reduce-scatter.9.cloned.1.call-start = ((), (), s32[]{:S(2)}) async-start(), calls=%async_computation.9 | async-start | bytes 7864320 | tf_op jit(solution)/shard_map/reduce_scatter | solution.py:170
  218.3 14.1 %copy-start.64 = (bf16[768,768]{1,0:T(8,128)(2,1)S(1)}, bf16[768,768]{1,0:T(8,128)(2,1)}, u32[]{:S(2)}) copy-start(bf16[768,768]{1,0:T(8,128)(2,1)} %param.30) | copy-start | bytes 3538948
  237.1 99.3 %reduce-scatter.7.cloned.1.call-start = ((), (), s32[]{:S(2)}) async-start(), calls=%async_computation.7 | async-start | bytes 3932160 | tf_op jit(solution)/shard_map/reduce_scatter | solution.py:153
  243.7 127.3 %all-gather.11.cloned.1.call-start = ((), (), s32[]{:S(2)}) async-start(), calls=%async_computation.10 | async-start | bytes 3932160 | tf_op jit(solution)/shard_map/all_gather | solution.py:181
  299.1 42.0 %copy-start.22 = (bf16[512,768]{1,0:T(8,128)(2,1)S(1)}, bf16[512,768]{1,0:T(8,128)(2,1)}, u32[]{:S(2)}) copy-start(bf16[512,768]{1,0:T(8,128)(2,1)} %param.21) | copy-start | bytes 2359300
  340.0 31.0 %copy-start.40 = (bf16[192,768]{1,0:T(8,128)(2,1)S(1)}, bf16[192,768]{1,0:T(8,128)(2,1)}, u32[]{:S(2)}) copy-start(bf16[192,768]{1,0:T(8,128)(2,1)} %param.26) | copy-start | bytes 884740
  340.0 34.0 %copy-start.52 = (f32[512]{0:T(512)}, f32[512]{0:T(512)S(1)}, u32[]{:S(2)}) copy-start(f32[512]{0:T(512)S(1)} %negate_multiply_fusion.1) | copy-start | bytes 6148
  342.3 165.6 %reduce-scatter.11.cloned.1.call-start = ((), (), s32[]{:S(2)}) async-start(), calls=%async_computation.11 | async-start | bytes 7864320 | tf_op jit(solution)/shard_map/reduce_scatter | solution.py:237
  376.9 7.7 %copy-start.14 = (bf16[2,1024,3,64]{1,3,2,0:T(8,128)(2,1)}, bf16[2,1024,3,64]{1,3,2,0:T(8,128)(2,1)S(1)}, u32[]{:S(2)}) copy-start(bf16[2,1024,3,64]{1,3,2,0:T(8,128)(2,1)S(1)} %get-tuple-element.484) | copy-start | bytes 2359300 | tf_op jit(solution)/shard_map/while
  378.9 8.7 %copy-start.43 = (pred[1024]{0:T(1024)(128)(4,1)}, pred[1024]{0:T(1024)(128)(4,1)S(1)}, u32[]{:S(2)}) copy-start(pred[1024]{0:T(1024)(128)(4,1)S(1)} %iota_compare_fusion.7) | copy-start | bytes 3076 | tf_op jit(solution)/shard_map/while
  404.9 7.7 %copy-start.14 = (bf16[2,1024,3,64]{1,3,2,0:T(8,128)(2,1)}, bf16[2,1024,3,64]{1,3,2,0:T(8,128)(2,1)S(1)}, u32[]{:S(2)}) copy-start(bf16[2,1024,3,64]{1,3,2,0:T(8,128)(2,1)S(1)} %get-tuple-element.484) | copy-start | bytes 2359300 | tf_op jit(solution)/shard_map/while
  406.9 8.7 %copy-start.43 = (pred[1024]{0:T(1024)(128)(4,1)}, pred[1024]{0:T(1024)(128)(4,1)S(1)}, u32[]{:S(2)}) copy-start(pred[1024]{0:T(1024)(128)(4,1)S(1)} %iota_compare_fusion.7) | copy-start | bytes 3076 | tf_op jit(solution)/shard_map/while
  444.3 17.9 %copy-start.24 = (bf16[2048,3,192]{0,2,1:T(8,128)(2,1)}, bf16[2048,3,192]{0,2,1:T(8,128)(2,1)S(1)}, u32[]{:S(2)}) copy-start(bf16[2048,3,192]{0,2,1:T(8,128)(2,1)S(1)} %constant_dynamic-update-slice_fusion) | copy-start | bytes 7077892
  448.9 297.3 %all-reduce.8.cloned.1.call-start = ((), (), s32[]{:S(2)}) async-start(), calls=%async_computation.12 | async-start | bytes 14155776 | tf_op jit(solution)/shard_map/psum | solution.py:250
  449.2 7.1 copy-start.63
  449.3 7.1 copy-start.69
  466.1 41.9 %copy-start.8 = (bf16[512,768]{1,0:T(8,128)(2,1)S(1)}, bf16[512,768]{1,0:T(8,128)(2,1)}, u32[]{:S(2)}) copy-start(bf16[512,768]{1,0:T(8,128)(2,1)} %param.19) | copy-start | bytes 2359300
  466.1 41.9 %copy-start.45 = (f32[768]{0:T(1024)S(1)}, f32[768]{0:T(1024)}, u32[]{:S(2)}) copy-start(f32[768]{0:T(1024)} %copy-done.44) | copy-start | bytes 9220
  466.1 41.8 %copy-start.47 = (f32[512]{0:T(512)S(1)}, f32[512]{0:T(512)}, u32[]{:S(2)}) copy-start(f32[512]{0:T(512)} %copy-done.46) | copy-start | bytes 6148
  466.1 43.8 %copy-start.51 = (f32[512]{0:T(512)S(1)}, f32[512]{0:T(512)}, u32[]{:S(2)}) copy-start(f32[512]{0:T(512)} %copy-done.50) | copy-start | bytes 6148
  466.2 43.8 %copy-start.49 = (f32[512]{0:T(512)S(1)}, f32[512]{0:T(512)}, u32[]{:S(2)}) copy-start(f32[512]{0:T(512)} %copy-done.48) | copy-start | bytes 6148
  466.8 44.0 %copy-start.13 = (f32[512,768]{1,0:T(8,128)S(1)}, f32[512,768]{1,0:T(8,128)}, u32[]{:S(2)}) copy-start(f32[512,768]{1,0:T(8,128)} %copy-done.12) | copy-start | bytes 4718596
  466.8 44.0 %copy-start.23 = (bf16[512,768]{1,0:T(8,128)(2,1)S(1)}, bf16[512,768]{1,0:T(8,128)(2,1)}, u32[]{:S(2)}) copy-start(bf16[512,768]{1,0:T(8,128)(2,1)} %param.21) | copy-start | bytes 2359300
  466.8 44.0 %copy-start.53 = (f32[512]{0:T(512)S(1)}, f32[512]{0:T(512)}, u32[]{:S(2)}) copy-start(f32[512]{0:T(512)} %copy-done.52) | copy-start | bytes 6148
  (65 other events, 144.4 us)
Sparse Core Ops, SparseCore 0:
  14.7 31.2 all-gather.4
  96.8 58.8 reduce-scatter.4
  159.8 28.4 all-gather.6
  189.8 28.4 all-gather.8
  237.2 58.8 reduce-scatter.8
  298.4 37.8 reduce-scatter.6
  342.5 28.4 all-gather.10
  449.1 58.8 reduce-scatter.10
  513.5 232.7 all-reduce.7
where the time goes:
time: 764 us; the launch traced here: 760 us
  waiting for transfers between devices  460 us (60%)
  matrix products  111 us (15%)
  blocking collectives  66 us (9%)
  local copies, waits for them, and re-layouts  61.2 us (8%)
  other arithmetic  44.7 us (6%)
  between operations  14.8 us (2%)
    psum x1, waiting for transfers between devices, local(): lax.psum((grad_w_qkv, grad_b_qkv, grad_w_out, grad_w_up, grad_b_up, grad_...  189 us
    reduce_scatter x1, waiting for transfers between devices, local(): lax.psum_scatter(jnp.dot(lax.slice_in_dim(attn_vals, 0, local_rows * lax....  57.6 us
    reduce_scatter x1, waiting for transfers between devices, local(): lax.psum_scatter(contract_last(lax.slice_in_dim(d_pre, 0, local_rows * la...  51.7 us
    psum x1, blocking collectives, local(): shared_sum = lax.psum(shared_local, ('dp', 'tensor'))  43.9 us
    reduce_scatter x1, waiting for transfers between devices, local(): lax.psum_scatter(jnp.dot(lax.slice_in_dim(act_low, 0, local_rows * lax.ax...  37.2 us
    all_gather x1, waiting for transfers between devices, local(): branch_all = lax.all_gather(d_branch, 'tensor', axis=0, tiled=True)  28.4 us
    all_gather x1, waiting for transfers between devices, local(): normed_all = lax.all_gather(normed_one_low, 'tensor', axis=0, tiled=True)  28.2 us
    all_gather x1, waiting for transfers between devices, local(): lax.all_gather(normed_two_low, 'tensor', axis=0, tiled=True)  28 us
  transfers between devices with their start and end apart: 9, of which 9 were waited for; matrix products, arithmetic and copies ran while one was open for 6% of the time, Pallas kernels for 0%

commit v1 on v0

--- a/solution.py
+++ b/solution.py
@@ -260,7 +260,8 @@
             jnp.sum(grad_out, axis=0),
         ]
     )
-    shared_sum = lax.psum(shared_local, ("dp", "tensor"))
+    parts = lax.all_gather(shared_local, ("dp", "tensor"), axis=0, tiled=False)
+    shared_sum = parts.sum(axis=0)
     return (
         output,
         grad_tokens,

time: 764 us -> 767 us (level)
    all_gather x0 -> x1, blocking collectives: none -> 48 us  [local(): parts = lax.all_gather(shared_local, ('dp', 'tensor'), axis=0, tiled=False)]
    psum x1 -> x0, blocking collectives: 43.9 us -> none  [local(): shared_sum = lax.psum(shared_local, ('dp', 'tensor'))]
where the time goes in v1:
time: 767 us; the launch traced here: 763 us
  waiting for transfers between devices  459 us (60%)
  matrix products  111 us (14%)
  blocking collectives  70.2 us (9%)
  local copies, waits for them, and re-layouts  61.2 us (8%)
  other arithmetic  44.7 us (6%)
  between operations  14.8 us (2%)
    psum x1, waiting for transfers between devices, local(): lax.psum((grad_w_qkv, grad_b_qkv, grad_w_out, grad_w_up, grad_b_up, grad_...  188 us
    reduce_scatter x1, waiting for transfers between devices, local(): lax.psum_scatter(jnp.dot(lax.slice_in_dim(attn_vals, 0, local_rows * lax....  57.6 us
    reduce_scatter x1, waiting for transfers between devices, local(): lax.psum_scatter(contract_last(lax.slice_in_dim(d_pre, 0, local_rows * la...  51.7 us
    all_gather x1, blocking collectives, local(): parts = lax.all_gather(shared_local, ('dp', 'tensor'), axis=0, tiled=False)  48 us
    reduce_scatter x1, waiting for transfers between devices, local(): lax.psum_scatter(jnp.dot(lax.slice_in_dim(act_low, 0, local_rows * lax.ax...  37.2 us
    all_gather x1, waiting for transfers between devices, local(): branch_all = lax.all_gather(d_branch, 'tensor', axis=0, tiled=True)  28.4 us
    all_gather x1, waiting for transfers between devices, local(): normed_all = lax.all_gather(normed_one_low, 'tensor', axis=0, tiled=True)  28.2 us
    all_gather x1, waiting for transfers between devices, local(): lax.all_gather(normed_two_low, 'tensor', axis=0, tiled=True)  28 us
  transfers between devices with their start and end apart: 9, of which 9 were waited for; matrix products, arithmetic and copies ran while one was open for 6% of the time, Pallas kernels for 0%

profile of v1, /device:TPU:0, one launch (start us, length us, event | category | flops | bytes accessed | tf_op | source)
XLA Modules:
  0.0 762.5 jit_solution(14221184813300642260)
XLA Ops:
  17.8 28.2 %all-gather.7.cloned.1.call-done = bf16[2048,768]{1,0:T(8,128)(2,1)} async-done(((bf16[512,768]{1,0:T(8,128)(2,1)}), bf16[2048,768]{1,0:T(8,128)(2,1)}) %all-gather.7.cloned.1.call-update) | async-done | bytes 3145744 | tf_op jit(solution)/shard_map/all_gather | solution.py:86
  46.0 3.9 fusion.118
  52.2 2.8 reshape_squeeze.8
  64.9 24.7 %while.28 = (s32[]{:T(128)}, bf16[2,1024,3,64]{1,3,2,0:T(8,128)(2,1)}, f32[2,3,1024]{2,1,0:T(4,128)}, bf16[2,1024,3,64]{1,3,2,0:T(8,128)(2,1)S(1)}, s32[2]{0:T(1...) while((s32[]{:T(128)}, ...), condition=%wide.region_7.8_spmd.clone, body=%wide.region_2.7_spmd.sunk.clone | while | flops 843842560 | bytes 47532784 | solution.py:126
  92.9 3.7 fusion.119
  98.0 57.6 %reduce-scatter.5.cloned.1.call-done = f32[512,768]{1,0:T(8,128)} async-done(((f32[2048,768]{1,0:T(8,128)}), f32[512,768]{1,0:T(8,128)}) %reduce-scatter.5.cloned.1.call-update) | async-done | bytes 1572880 | tf_op jit(solution)/shard_map/reduce_scatter | solution.py:130
  160.4 28.0 %all-gather.9.cloned.1.call-done = bf16[2048,768]{1,0:T(8,128)(2,1)} async-done(((bf16[512,768]{1,0:T(8,128)(2,1)}), bf16[2048,768]{1,0:T(8,128)(2,1)}) %all-gather.9.cloned.1.call-update) | async-done | bytes 3145744 | tf_op jit(solution)/shard_map/all_gather | solution.py:147
  188.4 7.5 fusion.120
  195.9 22.5 %all-gather.11.cloned.1.call-done = bf16[2048,768]{1,0:T(8,128)(2,1)} async-done(((bf16[512,768]{1,0:T(8,128)(2,1)}), bf16[2048,768]{1,0:T(8,128)(2,1)}) %all-gather.11.cloned.1.call-update) | async-done | bytes 3145744 | tf_op jit(solution)/shard_map/all_gather | solution.py:164
  218.3 12.4 %convert_reduce_fusion = (f32[768]{0:T(1024)}, bf16[2048,768]{1,0:T(8,128)(2,1)S(1)}, bf16[2048,768]{1,0:T(8,128)(2,1)}) fusion(f32[2048,768]{1,0:T(8,128)} %fusion.120, f32[768]{0:T(1024)S(1)} %convert_element_type.109, bf16[2048,768]{1,0:T(8,128)(2,1)} %all-gather.11.cloned.1.call-done, bf16[768,768]{1,0:T(8,128)(2,1)S(1)} %copy-done), kind=kOutput, calls=%fused_computation.112 | convolution fusion | flops 2455239936 | bytes 16914432 | tf_op jit(solution)/shard_map/dot_general | solution.py:45
  232.5 4.5 fusion.121
  237.1 6.5 convolution_convert_fusion
  244.3 51.7 %reduce-scatter.9.cloned.1.call-done = f32[512,768]{1,0:T(8,128)} async-done(((f32[2048,768]{1,0:T(8,128)}), f32[512,768]{1,0:T(8,128)}) %reduce-scatter.9.cloned.1.call-update) | async-done | bytes 1572880 | tf_op jit(solution)/shard_map/reduce_scatter | solution.py:170
  296.1 3.1 multiply_reduce_fusion.2
  299.2 37.2 %reduce-scatter.7.cloned.1.call-done = bf16[512,768]{1,0:T(8,128)(2,1)} async-done(((bf16[2048,768]{1,0:T(8,128)(2,1)}), bf16[512,768]{1,0:T(8,128)(2,1)}) %reduce-scatter.7.cloned.1.call-update) | async-done | bytes 786448 | tf_op jit(solution)/shard_map/reduce_scatter | solution.py:153
  336.4 3.7 fusion.110
  342.6 28.4 %all-gather.13.cloned.1.call-done = bf16[2048,768]{1,0:T(8,128)(2,1)} async-done(((bf16[512,768]{1,0:T(8,128)(2,1)}), bf16[2048,768]{1,0:T(8,128)(2,1)}) %all-gather.13.cloned.1.call-update) | async-done | bytes 3145744 | tf_op jit(solution)/shard_map/all_gather | solution.py:181
  371.0 3.1 convolution_convert_fusion.1
  376.9 56.3 %while.29 = (s32[]{:T(128)}, f32[2,1024,3,64]{1,3,2,0:T(8,128)}, f32[2,1024,3,64]{1,3,2,0:T(8,128)}, bf16[2,1024,3,64]{1,3,2,0:T(8,128)(2,1)S(1)}, bf16[2,1024,3...) while((s32[]{:T(128)}, f32[2,1024,3,64]{1,3,2,0:T(8,128)}, ...), condition=%wide.region_18.19_spmd.clone, body=%wide.region_15.18_spmd.sunk.clone | while | flops 2061432832 | bytes 165286976 | solution.py:223
  387.6 4.8 multiply_reduce_fusion.7
  392.5 4.0 multiply_convert_fusion.5
  415.7 4.8 multiply_reduce_fusion.7
  420.5 4.0 multiply_convert_fusion.5
  444.3 4.6 convolution_bitcast_fusion
  449.3 7.1 fusion.124
  456.3 4.2 fusion.123
  462.8 3.2 fusion.125
  469.0 22.1 %all-reduce.4 = (f32[3,192]{1,0:T(4,128)}, f32[768]{0:T(1024)}) all-reduce(f32[3,192]{1,0:T(4,128)S(1)} %convert_reduce_fusion.1, f32[768]{0:T(1024)S(1)} %copy-done.56), channel_id=1, replica_groups=mesh['dp'=8,'tensor'=4] {'dp'}, use_global_device_ids=true, to_apply=%region_31.32 | all-reduce | flops 1344 | bytes 10752 | tf_op jit(solution)/shard_map/psum | solution.py:250
  491.2 16.8 %reduce-scatter.11.cloned.1.call-done = f32[512,768]{1,0:T(8,128)} async-done(((f32[2048,768]{1,0:T(8,128)}), f32[512,768]{1,0:T(8,128)}) %reduce-scatter.11.cloned.1.call-update) | async-done | bytes 1572880 | tf_op jit(solution)/shard_map/reduce_scatter | solution.py:237
  512.6 48.0 %all-gather.1 = f32[32,6,768]{2,1,0:T(8,128)S(1)} all-gather(f32[1,6,768]{2,1,0:T(8,128)S(1)} %bitcast.262), channel_id=2, replica_groups=mesh['dp'=8,'tensor'=4] {'dp','tensor'}, dimensions={0}, use_global_device_ids=true | all-gather | bytes 608256 | tf_op jit(solution)/shard_map/all_gather | solution.py:263
  561.4 187.7 %all-reduce.8.cloned.1.call-done = (f32[768,3,192]{0,2,1:T(8,128)}, f32[192,768]{1,0:T(8,128)}, f32[768,768]{1,0:T(8,128)}, f32[768,768]{1,0:T(8,128)}) async-done(((f32[768,3,192]{0,2,1:T(8,128)}, f32[192,768]{1,0:T(8,128)}, f32[768,768]{1,0:T(8,128)}, f32[768,768]{1,0:T(8,128)}), (f32[768,3,192]{0,2,1:T(8,128)}, f32[192,768]{1,0:T(8,128)}, f32[768,768]{1,0:T(8,128)}, ...) | async-done | bytes 7077904 | tf_op jit(solution)/shard_map/psum | solution.py:250
  749.1 2.9 copy.108
  (315 shorter events, 127.3 us)
Async XLA Ops:
  7.2 211.2 %copy-start = (bf16[768,768]{1,0:T(8,128)(2,1)S(1)}, bf16[768,768]{1,0:T(8,128)(2,1)}, u32[]{:S(2)}) copy-start(bf16[768,768]{1,0:T(8,128)(2,1)} %param.32) | copy-start | bytes 3538948
  7.2 7.5 copy-start.57
  7.2 38.8 %copy-start.65 = (bf16[768,3,192]{0,2,1:T(8,128)(2,1)S(1)}, bf16[768,3,192]{0,2,1:T(8,128)(2,1)}, u32[]{:S(2)}) copy-start(bf16[768,3,192]{0,2,1:T(8,128)(2,1)} %param.24) | copy-start | bytes 2654212
  7.2 38.8 %all-gather.7.cloned.1.call-start = ((), (), s32[]{:S(2)}) async-start(), calls=%async_computation.4 | async-start | bytes 3932160 | tf_op jit(solution)/shard_map/all_gather | solution.py:86
  14.6 141.1 %reduce-scatter.5.cloned.1.call-start = ((), (), s32[]{:S(2)}) async-start(), calls=%async_computation.5 | async-start | bytes 7864320 | tf_op jit(solution)/shard_map/reduce_scatter | solution.py:130
  96.6 59.0 %copy-start.7 = (bf16[512,768]{1,0:T(8,128)(2,1)S(1)}, bf16[512,768]{1,0:T(8,128)(2,1)}, u32[]{:S(2)}) copy-start(bf16[512,768]{1,0:T(8,128)(2,1)} %param.19) | copy-start | bytes 2359300
  96.7 91.7 %all-gather.9.cloned.1.call-start = ((), (), s32[]{:S(2)}) async-start(), calls=%async_computation.6 | async-start | bytes 3932160 | tf_op jit(solution)/shard_map/all_gather | solution.py:147
  159.7 58.6 %all-gather.11.cloned.1.call-start = ((), (), s32[]{:S(2)}) async-start(), calls=%async_computation.8 | async-start | bytes 3932160 | tf_op jit(solution)/shard_map/all_gather | solution.py:164
  160.3 135.8 %reduce-scatter.9.cloned.1.call-start = ((), (), s32[]{:S(2)}) async-start(), calls=%async_computation.9 | async-start | bytes 7864320 | tf_op jit(solution)/shard_map/reduce_scatter | solution.py:170
  218.3 14.1 %copy-start.64 = (bf16[768,768]{1,0:T(8,128)(2,1)S(1)}, bf16[768,768]{1,0:T(8,128)(2,1)}, u32[]{:S(2)}) copy-start(bf16[768,768]{1,0:T(8,128)(2,1)} %param.30) | copy-start | bytes 3538948
  237.1 99.3 %reduce-scatter.7.cloned.1.call-start = ((), (), s32[]{:S(2)}) async-start(), calls=%async_computation.7 | async-start | bytes 3932160 | tf_op jit(solution)/shard_map/reduce_scatter | solution.py:153
  243.7 127.3 %all-gather.13.cloned.1.call-start = ((), (), s32[]{:S(2)}) async-start(), calls=%async_computation.10 | async-start | bytes 3932160 | tf_op jit(solution)/shard_map/all_gather | solution.py:181
  299.1 42.0 %copy-start.22 = (bf16[512,768]{1,0:T(8,128)(2,1)S(1)}, bf16[512,768]{1,0:T(8,128)(2,1)}, u32[]{:S(2)}) copy-start(bf16[512,768]{1,0:T(8,128)(2,1)} %param.21) | copy-start | bytes 2359300
  340.0 31.0 %copy-start.40 = (bf16[192,768]{1,0:T(8,128)(2,1)S(1)}, bf16[192,768]{1,0:T(8,128)(2,1)}, u32[]{:S(2)}) copy-start(bf16[192,768]{1,0:T(8,128)(2,1)} %param.26) | copy-start | bytes 884740
  340.0 34.0 %copy-start.52 = (f32[512]{0:T(512)}, f32[512]{0:T(512)S(1)}, u32[]{:S(2)}) copy-start(f32[512]{0:T(512)S(1)} %negate_multiply_fusion.1) | copy-start | bytes 6148
  342.3 165.6 %reduce-scatter.11.cloned.1.call-start = ((), (), s32[]{:S(2)}) async-start(), calls=%async_computation.11 | async-start | bytes 7864320 | tf_op jit(solution)/shard_map/reduce_scatter | solution.py:237
  376.9 7.7 %copy-start.14 = (bf16[2,1024,3,64]{1,3,2,0:T(8,128)(2,1)}, bf16[2,1024,3,64]{1,3,2,0:T(8,128)(2,1)S(1)}, u32[]{:S(2)}) copy-start(bf16[2,1024,3,64]{1,3,2,0:T(8,128)(2,1)S(1)} %get-tuple-element.501) | copy-start | bytes 2359300 | tf_op jit(solution)/shard_map/while
  378.9 8.7 %copy-start.43 = (pred[1024]{0:T(1024)(128)(4,1)}, pred[1024]{0:T(1024)(128)(4,1)S(1)}, u32[]{:S(2)}) copy-start(pred[1024]{0:T(1024)(128)(4,1)S(1)} %iota_compare_fusion.7) | copy-start | bytes 3076 | tf_op jit(solution)/shard_map/while
  404.9 7.7 %copy-start.14 = (bf16[2,1024,3,64]{1,3,2,0:T(8,128)(2,1)}, bf16[2,1024,3,64]{1,3,2,0:T(8,128)(2,1)S(1)}, u32[]{:S(2)}) copy-start(bf16[2,1024,3,64]{1,3,2,0:T(8,128)(2,1)S(1)} %get-tuple-element.501) | copy-start | bytes 2359300 | tf_op jit(solution)/shard_map/while
  406.9 8.7 %copy-start.43 = (pred[1024]{0:T(1024)(128)(4,1)}, pred[1024]{0:T(1024)(128)(4,1)S(1)}, u32[]{:S(2)}) copy-start(pred[1024]{0:T(1024)(128)(4,1)S(1)} %iota_compare_fusion.7) | copy-start | bytes 3076 | tf_op jit(solution)/shard_map/while
  444.3 17.9 %copy-start.24 = (bf16[2048,3,192]{0,2,1:T(8,128)(2,1)}, bf16[2048,3,192]{0,2,1:T(8,128)(2,1)S(1)}, u32[]{:S(2)}) copy-start(bf16[2048,3,192]{0,2,1:T(8,128)(2,1)S(1)} %constant_dynamic-update-slice_fusion) | copy-start | bytes 7077892
  448.9 300.2 %all-reduce.8.cloned.1.call-start = ((), (), s32[]{:S(2)}) async-start(), calls=%async_computation.12 | async-start | bytes 14155776 | tf_op jit(solution)/shard_map/psum | solution.py:250
  449.2 7.1 copy-start.63
  449.3 7.1 copy-start.69
  466.1 41.9 %copy-start.8 = (bf16[512,768]{1,0:T(8,128)(2,1)S(1)}, bf16[512,768]{1,0:T(8,128)(2,1)}, u32[]{:S(2)}) copy-start(bf16[512,768]{1,0:T(8,128)(2,1)} %param.19) | copy-start | bytes 2359300
  466.1 41.9 %copy-start.45 = (f32[768]{0:T(1024)S(1)}, f32[768]{0:T(1024)}, u32[]{:S(2)}) copy-start(f32[768]{0:T(1024)} %copy-done.44) | copy-start | bytes 9220
  466.1 41.8 %copy-start.47 = (f32[512]{0:T(512)S(1)}, f32[512]{0:T(512)}, u32[]{:S(2)}) copy-start(f32[512]{0:T(512)} %copy-done.46) | copy-start | bytes 6148
  466.1 43.8 %copy-start.51 = (f32[512]{0:T(512)S(1)}, f32[512]{0:T(512)}, u32[]{:S(2)}) copy-start(f32[512]{0:T(512)} %copy-done.50) | copy-start | bytes 6148
  466.2 43.8 %copy-start.49 = (f32[512]{0:T(512)S(1)}, f32[512]{0:T(512)}, u32[]{:S(2)}) copy-start(f32[512]{0:T(512)} %copy-done.48) | copy-start | bytes 6148
  466.8 44.0 %copy-start.13 = (f32[512,768]{1,0:T(8,128)S(1)}, f32[512,768]{1,0:T(8,128)}, u32[]{:S(2)}) copy-start(f32[512,768]{1,0:T(8,128)} %copy-done.12) | copy-start | bytes 4718596
  466.8 44.0 %copy-start.23 = (bf16[512,768]{1,0:T(8,128)(2,1)S(1)}, bf16[512,768]{1,0:T(8,128)(2,1)}, u32[]{:S(2)}) copy-start(bf16[512,768]{1,0:T(8,128)(2,1)} %param.21) | copy-start | bytes 2359300
  466.8 44.0 %copy-start.53 = (f32[512]{0:T(512)S(1)}, f32[512]{0:T(512)}, u32[]{:S(2)}) copy-start(f32[512]{0:T(512)} %copy-done.52) | copy-start | bytes 6148
  (65 other events, 144.4 us)
Sparse Core Ops, SparseCore 0:
  14.7 31.2 all-gather.6
  96.8 58.8 reduce-scatter.4
  159.8 28.4 all-gather.8
  189.8 28.4 all-gather.10
  237.2 58.8 reduce-scatter.8
  298.4 37.8 reduce-scatter.6
  342.5 28.4 all-gather.12
  449.1 58.8 reduce-scatter.10
  513.5 235.5 all-reduce.7
